TPU v7x, 256 devices: a whole 4x4x8 slice. The times are simulated.
256 devices in a mesh: gx: 16 (over z, core), gy: 4 (over x), gz: 4 (over y).
Axes of the slice: x: 4, y: 4, z: 8, core: 2. Of those that a mesh axis runs over, the one named last changes fastest.
Arguments:
- block_values: bfloat16 [4, 64, 4, 6, 128, 128], P('gy', 'gx', 'gz'), as said below
- block_cols: int32 [4, 64, 4, 6], P('gy', 'gx', 'gz'), may hold values from 0 to 63, as said below
Outputs:
- purified: float32 [2048, 32768], P(('gx', 'gy'), 'gz')
Inputs may be any that keep to these rules, and one draw needn't show every extreme that they name: block_cols[a, s, b, :] holds 6 distinct tile columns of panel b at which tile row a * 64 + s of P is nonzero; every tile column of a panel is listed by exactly 6 tile rows of each slab; the pattern is symmetric: tile (i, j) is listed exactly when tile (j, i) is. `block_values`: P is symmetric: the tile listed at (i, j) is the transpose of the tile listed at (j, i), and diagonal tiles are symmetric.
All inputs are finite; a program needn't handle non-finite values.
Results may differ from a plain program's by a relative error of at most 0.0033.
Values may be sent and summed in bfloat16 or wider, within the bound.
A program may use at most 128 MiB of HBM per device.

v0:
```python
import jax
import jax.numpy as jnp
from jax import lax
from jax.sharding import PartitionSpec as P

WIN = 1


def picked_2(x, axis, root):
    return lax.dynamic_index_in_dim(lax.all_gather(x, axis), root, 0, keepdims=False)


def in_blocks(x, dim, length):
    lengths = x.shape
    tiles = x.reshape(*lengths[:dim], length, lengths[dim] // length, *lengths[dim + 1 :])
    return jnp.moveaxis(tiles, dim, 0)


def sent_and_summed(x, axis, dim):
    tiles = in_blocks(x, dim, lax.axis_size(axis))
    arrived = lax.all_to_all(tiles, axis, split_axis=0, concat_axis=0, tiled=True)
    return arrived.astype(jnp.float32).sum(axis=0)


def densify(left_tiles, left_columns, slab_tiles):
    onehot = (
        left_columns[:, :, None] == jnp.arange(slab_tiles, dtype=jnp.int32)[None, None, :]
    ).astype(jnp.bfloat16)
    densified = jnp.einsum("wkj,wkyx->wyjx", onehot, left_tiles, preferred_element_type=jnp.float32)
    tile_size = left_tiles.shape[2]
    return densified.astype(jnp.bfloat16).reshape(
        left_tiles.shape[0] * tile_size, slab_tiles, tile_size
    )


def product_one(left_panel, panel_tiles, panel_columns):
    summed = jnp.zeros(
        (left_panel.shape[0], panel_tiles.shape[0], panel_tiles.shape[2]), jnp.float32
    )
    for column_slot in range(panel_tiles.shape[1]):
        picked = jnp.take(left_panel, panel_columns[:, column_slot], axis=1)
        summed = summed + jnp.einsum(
            "rix,iyx->riy", picked, panel_tiles[:, column_slot], preferred_element_type=jnp.float32
        )
    return summed


def product_two(rounded, panel_tiles, panel_columns, panel_width):
    summed = jnp.zeros((rounded.shape[0], panel_width, panel_tiles.shape[3]), jnp.float32)
    for column_slot in range(panel_tiles.shape[1]):
        product = jnp.einsum(
            "rix,ixy->riy", rounded, panel_tiles[:, column_slot], preferred_element_type=jnp.float32
        )
        summed = summed.at[:, panel_columns[:, column_slot], :].add(product)
    return summed


def local(block_values, block_cols):
    tiles_here = block_values[0, :, 0]
    columns_here = block_cols[0, :, 0]
    tile_size = tiles_here.shape[2]
    slab_tiles = tiles_here.shape[0] * lax.axis_size("gx")
    left_tiles, left_columns = (
        picked_2(tiles_here[:WIN], "gy", 0),
        picked_2(columns_here[:WIN], "gy", 0),
    )
    left_panel = densify(left_tiles, left_columns, slab_tiles)
    height = left_panel.shape[0]
    on_diagonal = (lax.axis_index("gy") == lax.axis_index("gz")).astype(jnp.float32)
    panel_tiles, panel_columns = (
        lax.all_gather(tiles_here, "gx", axis=0, tiled=True),
        lax.all_gather(columns_here, "gx", axis=0, tiled=True),
    )
    partial_square = product_one(left_panel, panel_tiles, panel_columns)
    partial_square = partial_square.reshape(height, slab_tiles * tile_size)
    square = lax.psum(partial_square, "gz")
    square_low = square.astype(jnp.bfloat16).reshape(height, slab_tiles, tile_size)
    applied = product_two(square_low, panel_tiles, panel_columns, slab_tiles).reshape(
        height // lax.axis_size("gy") * lax.axis_size("gy"), slab_tiles * tile_size
    )
    return sent_and_summed(
        (3.0 * on_diagonal * square - 2.0 * applied).astype(jnp.bfloat16), "gy", 0
    )


def solution(mesh):
    in_specs = (P("gy", "gx", "gz", None, None, None), P("gy", "gx", "gz", None))
    out_specs = P(("gx", "gy"), "gz")
    return jax.shard_map(local, mesh=mesh, in_specs=in_specs, out_specs=out_specs, check_vma=False)
```

profile of v0, /device:TPU:32, one launch (start us, length us, event | category | flops | bytes accessed | tf_op | source)
XLA Modules:
  0.0 381.8 jit_solution(5912386459244780532)
XLA Ops:
  6.5 0.0 all-gather.6.cloned.1.call-start
  6.5 2.2 copy.30
  8.7 0.0 all-gather.6.cloned.1.call-update
  8.7 0.0 all-reduce.2.cloned.1.call-start
  8.8 9.7 %all-gather = s32[4,1,1,6]{3,2,1,0:T(1,128)S(1)} all-gather(s32[1,1,1,6]{3,2,1,0:T(1,128)S(1)} %slice-done.4), channel_id=2, replica_groups=mesh['gx'=16,'gy'=4,'gz'=4] {'gy'}, dimensions={0}, use_global_device_ids=true | all-gather | bytes 120 | tf_op jit(solution)/shard_map/all_gather | solution.py:10
  18.5 13.3 %all-gather.1 = bf16[4,1,1,6,128,128]{5,4,3,2,1,0:T(8,128)(2,1)S(1)} all-gather(bf16[1,1,1,6,128,128]{5,4,3,2,1,0:T(8,128)(2,1)S(1)} %slice-done.3), channel_id=3, replica_groups=mesh['gx'=16,'gy'=4,'gz'=4] {'gy'}, dimensions={0}, use_global_device_ids=true | all-gather | bytes 983040 | tf_op jit(solution)/shard_map/all_gather | solution.py:10
  31.8 0.8 convert_bitcast_fusion
  32.7 0.0 copy-start.5
  32.7 1.4 copy.29
  34.0 0.0 copy-done.5
  34.1 18.6 %all-gather.2 = s32[1,64,1,6]{3,2,0,1:T(1,128)S(1)} all-gather(s32[1,4,1,6]{3,2,0,1:T(1,128)S(1)} %bitcast.101), channel_id=4, replica_groups=mesh['gx'=16,'gy'=4,'gz'=4] {'gx'}, dimensions={1}, use_global_device_ids=true | all-gather | bytes 1632 | tf_op jit(solution)/shard_map/all_gather | solution.py:72
  52.7 0.4 fusion.41
  53.1 2.2 gather_fusion
  55.3 2.1 gather_fusion.4
  57.4 2.2 gather_fusion.3
  59.6 2.1 gather_fusion.2
  61.7 2.2 gather_fusion.1
  63.9 2.1 gather_fusion.5
  66.1 19.6 %all-gather.6.cloned.1.call-done = bf16[1,64,1,6,128,128]{5,4,1,3,2,0:T(8,128)(2,1)} async-done(((bf16[1,4,1,6,128,128]{5,4,1,3,2,0:T(8,128)(2,1)}), bf16[1,64,1,6,128,128]{5,4,1,3,2,0:T(8,128)(2,1)}) %all-gather.6.cloned.1.call-update) | async-done | bytes 12582928 | tf_op jit(solution)/shard_map/all_gather | solution.py:71
  85.7 6.2 %fusion.10 = f32[64,128,128]{1,2,0:T(8,128)} fusion(bf16[64,128,128]{2,1,0:T(8,128)(2,1)} %gather_fusion, pred[64]{0:T(512)(128)(4,1)S(1)} %get-tuple-element.29, bf16[64,6,128,128]{3,2,0,1:T(8,128)(2,1)} %bitcast.84), kind=kOutput, calls=%fused_computation.31 | convolution fusion | flops 269484032 | bytes 8388672 | tf_op jit(solution)/shard_map/rix,iyx->riy/dot_general | solution.py:42
  91.8 6.0 %fusion.2 = f32[64,128,128]{1,2,0:T(8,128)} fusion(bf16[64,128,128]{2,1,0:T(8,128)(2,1)} %gather_fusion.4, pred[64]{0:T(512)(128)(4,1)S(1)} %get-tuple-element.25, bf16[64,6,128,128]{3,2,0,1:T(8,128)(2,1)} %bitcast.85), kind=kOutput, calls=%fused_computation.23 | convolution fusion | flops 269484032 | bytes 8388672 | tf_op jit(solution)/shard_map/rix,iyx->riy/dot_general | solution.py:42
  97.8 3.6 fusion.4
  101.5 3.6 fusion.6
  105.1 3.6 fusion.8
  108.7 10.1 %add_add_fusion = f32[64,128,128]{1,2,0:T(8,128)} fusion(f32[64,128,128]{1,2,0:T(8,128)} %fusion.2, f32[64,128,128]{1,2,0:T(8,128)} %fusion.4, f32[64,128,128]{1,2,0:T(8,128)} %fusion.6, f32[64,128,128]{1,2,0:T(8,128)} %fusion.10, f32[64,128,128]{1,2,0:T(8,128)} %fusion.8, bf16[64,128,128]{2,1,0:T(8,128)(2,1)S(1)} %copy-done.4, ...), kind=kOutput, calls=%fused_computation.15 | convolution fusion | flops 274726912 | bytes 29360640 | tf_op jit(solution)/shard_map/rix,iyx->riy/dot_general | solution.py:42
  118.8 0.0 all-reduce.2.cloned.1.call-update
  118.8 98.5 %all-reduce.2.cloned.1.call-done = f32[128,8192]{0,1:T(8,128)} async-done(((f32[128,8192]{0,1:T(8,128)}), f32[128,8192]{0,1:T(8,128)}) %all-reduce.2.cloned.1.call-update) | async-done | bytes 4194320 | tf_op jit(solution)/shard_map/psum | solution.py:76
  217.4 2.5 convert_element_type.27
  219.9 0.0 slice-start.1
  219.9 4.6 %fusion.24 = f32[64,128,128]{2,1,0:T(8,128)} fusion(bf16[128,64,128]{0,2,1:T(8,128)(2,1)S(1)} %bitcast.78, bf16[64,6,128,128]{3,2,0,1:T(8,128)(2,1)} %bitcast.86), kind=kOutput, calls=%fused_computation.47 | convolution fusion | flops 268435456 | bytes 8388608 | tf_op jit(solution)/shard_map/rix,ixy->riy/dot_general | solution.py:51
  224.5 4.6 %fusion.25 = f32[64,128,128]{2,1,0:T(8,128)} fusion(bf16[128,64,128]{0,2,1:T(8,128)(2,1)S(1)} %bitcast.79, bf16[64,6,128,128]{3,2,0,1:T(8,128)(2,1)} %bitcast.87), kind=kOutput, calls=%fused_computation.48 | convolution fusion | flops 268435456 | bytes 8388608 | tf_op jit(solution)/shard_map/rix,ixy->riy/dot_general | solution.py:51
  229.1 2.8 fusion.26
  231.9 2.8 fusion.27
  234.7 2.8 fusion.28
  237.5 2.8 fusion.29
  240.3 2.5 broadcast_in_dim.11
  242.8 13.7 %scatter_fusion = f32[128,64,128]{2,0,1:T(8,128)} fusion(f32[128,64,128]{2,0,1:T(8,128)} %broadcast_in_dim.11, s32[64]{0:T(128)S(1)} %get-tuple-element.7, f32[64,128,128]{2,1,0:T(8,128)} %fusion.24), kind=kCustom, calls=%fused_computation.6 | custom fusion | flops 1048576 | bytes 12583168 | tf_op jit(solution)/shard_map/scatter-add | solution.py:54
  256.5 13.7 %scatter_fusion.1 = f32[128,64,128]{2,0,1:T(8,128)} fusion(f32[128,64,128]{2,0,1:T(8,128)} %scatter_fusion, s32[64]{0:T(128)S(1)} %get-tuple-element.8, f32[64,128,128]{2,1,0:T(8,128)} %fusion.25), kind=kCustom, calls=%fused_computation.7 | custom fusion | flops 1048576 | bytes 12583168 | tf_op jit(solution)/shard_map/scatter-add | solution.py:54
  270.2 13.7 %scatter_fusion.2 = f32[128,64,128]{2,0,1:T(8,128)} fusion(f32[128,64,128]{2,0,1:T(8,128)} %scatter_fusion.1, s32[64]{0:T(128)S(1)} %get-tuple-element.9, f32[64,128,128]{2,1,0:T(8,128)} %fusion.26), kind=kCustom, calls=%fused_computation.8 | custom fusion | flops 1048576 | bytes 12583168 | tf_op jit(solution)/shard_map/scatter-add | solution.py:54
  283.9 13.6 %scatter_fusion.3 = f32[128,64,128]{2,0,1:T(8,128)} fusion(f32[128,64,128]{2,0,1:T(8,128)} %scatter_fusion.2, s32[64]{0:T(128)S(1)} %get-tuple-element.10, f32[64,128,128]{2,1,0:T(8,128)} %fusion.27), kind=kCustom, calls=%fused_computation.9 | custom fusion | flops 1048576 | bytes 12583168 | tf_op jit(solution)/shard_map/scatter-add | solution.py:54
  297.5 13.7 %scatter_fusion.4 = f32[128,64,128]{2,0,1:T(8,128)} fusion(f32[128,64,128]{2,0,1:T(8,128)} %scatter_fusion.3, s32[64]{0:T(128)S(1)} %get-tuple-element.11, f32[64,128,128]{2,1,0:T(8,128)} %fusion.28), kind=kCustom, calls=%fused_computation.10 | custom fusion | flops 1048576 | bytes 12583168 | tf_op jit(solution)/shard_map/scatter-add | solution.py:54
  311.1 13.6 %scatter_fusion.5 = f32[128,64,128]{2,0,1:T(8,128)} fusion(f32[128,64,128]{2,0,1:T(8,128)} %scatter_fusion.4, s32[64]{0:T(128)S(1)} %get-tuple-element.6, f32[64,128,128]{2,1,0:T(8,128)} %fusion.29), kind=kCustom, calls=%fused_computation.11 | custom fusion | flops 1048576 | bytes 12583168 | tf_op jit(solution)/shard_map/scatter-add | solution.py:54
  324.8 4.7 %broadcast_multiply_fusion = f32[128,64,128]{2,0,1:T(8,128)} fusion(f32[128,64,128]{2,0,1:T(8,128)} %scatter_fusion.5), kind=kLoop, calls=%fused_computation.39 | loop fusion | flops 1048576 | bytes 8388608 | tf_op jit(solution)/shard_map/mul | solution.py:82
  329.5 5.6 %copy.42 = f32[128,64,128]{0,2,1:T(8,128)} copy(f32[128,64,128]{2,0,1:T(8,128)} %broadcast_multiply_fusion) | data formatting | bytes 8388608 | tf_op jit(solution)/shard_map/mul | solution.py:82
  335.1 5.2 %fusion = bf16[128,8192]{0,1:T(8,128)(2,1)} fusion(f32[128,64,128]{0,2,1:T(8,128)} %copy.42, f32[128,8192]{0,1:T(8,128)} %all-reduce.2.cloned.1.call-done, f32[]{:T(128)S(6)} %mul_shard_map.3), kind=kLoop, calls=%fused_computation.13 | loop fusion | flops 3145728 | bytes 10485764 | tf_op jit(solution)/shard_map/convert_element_type | solution.py:82
  340.3 2.9 copy.43
  343.3 30.4 %all_to_all.5 = bf16[4,32,8192]{2,1,0:T(8,128)(2,1)S(1)} all-to-all(bf16[4,32,8192]{2,1,0:T(8,128)(2,1)S(1)} %bitcast.99), channel_id=1, replica_groups=mesh['gx'=16,'gy'=4,'gz'=4] {'gy'}, dimensions={0} | all-to-all | bytes 4194304 | tf_op jit(solution)/shard_map/all_to_all | solution.py:21
  373.6 1.3 convert_reduce_fusion
  (34 shorter events, 0.1 us)
Async XLA Ops:
  6.5 12.0 %slice-start.3 = ((bf16[1,4,1,6,128,128]{5,4,3,2,1,0:T(8,128)(2,1)}), bf16[1,1,1,6,128,128]{5,4,3,2,1,0:T(8,128)(2,1)S(1)}, s32[]{:S(2)}) async-start(bf16[1,4,1,6,128,128]{5,4,3,2,1,0:T(8,128)(2,1)} %param.4), calls=%async_computation.6 | async-start | bytes 393216 | tf_op jit(solution)/shard_map/slice | solution.py:64
  6.5 2.2 slice-start.4
  6.5 79.1 %all-gather.6.cloned.1.call-start = ((), (), s32[]{:S(2)}) async-start(), calls=%async_computation.2 | async-start | bytes 13369344 | tf_op jit(solution)/shard_map/all_gather | solution.py:71
  8.7 208.6 %all-reduce.2.cloned.1.call-start = ((), (), s32[]{:S(2)}) async-start(), calls=%async_computation.1 | async-start | bytes 8388608 | tf_op jit(solution)/shard_map/psum | solution.py:76
  32.7 1.4 copy-start.5
  85.7 12.2 %copy-start = (bf16[1,64,1,6,128,128]{5,4,1,3,2,0:T(8,128)(2,1)S(1)}, bf16[1,64,1,6,128,128]{5,4,1,3,2,0:T(8,128)(2,1)}, u32[]{:S(2)}) copy-start(bf16[1,64,1,6,128,128]{5,4,1,3,2,0:T(8,128)(2,1)} %all-gather.6.cloned.1.call-done) | copy-start | bytes 37748740
  91.8 6.0 %copy-start.1 = (bf16[64,128,128]{2,1,0:T(8,128)(2,1)S(1)}, bf16[64,128,128]{2,1,0:T(8,128)(2,1)}, u32[]{:S(2)}) copy-start(bf16[64,128,128]{2,1,0:T(8,128)(2,1)} %gather_fusion.3) | copy-start | bytes 6291460
  97.8 3.6 copy-start.2
  101.5 3.6 copy-start.3
  105.1 3.6 copy-start.4
  217.4 11.7 %slice-start = ((s8[12582912]{0:T(1024)(128)(4,1)}), s8[4194304]{0:T(1024)(128)(4,1)S(1)}, s32[]{:S(2)}) async-start(s8[12582912]{0:T(1024)(128)(4,1)} %bitcast.92), calls=%async_computation.3 | async-start | bytes 8388608
  219.9 9.2 %slice-start.1 = ((s8[12582912]{0:T(1024)(128)(4,1)}), s8[4194304]{0:T(1024)(128)(4,1)S(1)}, s32[]{:S(2)}) async-start(s8[12582912]{0:T(1024)(128)(4,1)} %bitcast.92), calls=%async_computation.4 | async-start | bytes 8388608
  224.5 4.6 %slice-start.2 = ((s8[12582912]{0:T(1024)(128)(4,1)}), s8[4194304]{0:T(1024)(128)(4,1)S(1)}, s32[]{:S(2)}) async-start(s8[12582912]{0:T(1024)(128)(4,1)} %bitcast.92), calls=%async_computation.5 | async-start | bytes 8388608
Sparse Core Ops, SparseCore 0:
  9.2 76.4 all-gather.5
  118.9 98.3 all-reduce.1
where the time goes:
time: 383 us; the launch traced here: 382 us
  waiting for transfers between devices  118 us (31%)
  other arithmetic  96.3 us (25%)
  blocking collectives  72 us (19%)
  matrix products  54.3 us (14%)
  local copies, waits for them, and re-layouts  27.4 us (7%)
  between operations  13.5 us (4%)
    psum x1, waiting for transfers between devices, local(): square = lax.psum(partial_square, 'gz')  98.5 us
    scatter-add x6, other arithmetic, product_two(): summed = summed.at[:, panel_columns[:, column_slot], :].add(product)  82 us
    dot_general x6, matrix products, product_one(): jnp.einsum('rix,iyx->riy', picked, panel_tiles[:, column_slot], preferred...  33.1 us
    all_to_all x1, blocking collectives, sent_and_summed(): lax.all_to_all(tiles, axis, split_axis=0, concat_axis=0, tiled=True)  30.4 us
    all_gather x2, blocking collectives, picked_2(): lax.all_gather(x, axis)  23 us
    dot_general x6, matrix products, product_two(): jnp.einsum('rix,ixy->riy', rounded, panel_tiles[:, column_slot], preferre...  20.4 us
    all_gather x1, waiting for transfers between devices, local(): lax.all_gather(tiles_here, 'gx', axis=0, tiled=True)  19.6 us
    all_gather x1, blocking collectives, local(): lax.all_gather(columns_here, 'gx', axis=0, tiled=True)  18.6 us
  transfers between devices with their start and end apart: 2, of which 2 were waited for; matrix products, arithmetic and copies ran while one was open for 4% of the time, Pallas kernels for 0%

commit v1 on v0

--- a/solution.py
+++ b/solution.py
@@ -4,6 +4,12 @@
 from jax.sharding import PartitionSpec as P
 
 WIN = 1
+
+
+def reach_shifts_all_all(w_in, mesh_dim):
+    x_next = jnp.stack([w_in] * jax.lax.axis_size(mesh_dim))
+    piece_now = jax.lax.all_to_all(x_next, split_axis=0, concat_axis=0, axis_name=mesh_dim)
+    return jnp.concatenate(piece_now, 0)
 
 
 def picked_2(x, axis, root):
@@ -68,7 +74,7 @@
     height = left_panel.shape[0]
     on_diagonal = (lax.axis_index("gy") == lax.axis_index("gz")).astype(jnp.float32)
     panel_tiles, panel_columns = (
-        lax.all_gather(tiles_here, "gx", axis=0, tiled=True),
+        reach_shifts_all_all(tiles_here, "gx"),
         lax.all_gather(columns_here, "gx", axis=0, tiled=True),
     )
     partial_square = product_one(left_panel, panel_tiles, panel_columns)

time: 383 us -> 619 us (1.62)
  blocking collectives: 72 us -> 310 us
  waiting for transfers between devices: 118 us -> 99.3 us
  local copies, waits for them, and re-layouts: 27.4 us -> 41.7 us
  starting transfers between devices: 0.04 us -> 8.76 us
  matrix products: 54.3 us -> 47.9 us
    all_gather x1, blocking collectives: 18.6 us -> 256 us  [local(): lax.all_gather(columns_here, 'gx', axis=0, tiled=True)]
    all_gather x1 -> x0, waiting for transfers between devices: 19.6 us -> none  [local(): lax.all_gather(tiles_here, 'gx', axis=0, tiled=True)]
    another operation x0 -> x2, local copies, waits for them, and re-layouts: none -> 8.86 us  [reach_shifts_all_all(): x_next = jnp.stack([w_in] * jax.lax.axis_size(mesh_dim))]
    all_to_all x0 -> x1, starting transfers between devices: none -> 8.72 us  [reach_shifts_all_all(): jax.lax.all_to_all(x_next, split_axis=0, concat_axis=0, axis_name=mesh_dim)]
    all_to_all x0 -> x1, local copies, waits for them, and re-layouts: none -> 6.63 us  [reach_shifts_all_all(): jax.lax.all_to_all(x_next, split_axis=0, concat_axis=0, axis_name=mesh_dim)]
  transfers between devices with their start and end apart: 2 -> 2, of which waited for: 2 -> 1; matrix products, arithmetic and copies ran while one was open for 4% -> 3% of each run, Pallas kernels for 0% -> 0%
where the time goes in v1:
time: 619 us; the launch traced here: 618 us
  blocking collectives  310 us (50%)
  waiting for transfers between devices  99.3 us (16%)
  other arithmetic  96.3 us (16%)
  matrix products  47.9 us (8%)
  local copies, waits for them, and re-layouts  41.7 us (7%)
  between operations  13.6 us (2%)
  starting transfers between devices  8.76 us (1%)
    all_gather x1, blocking collectives, local(): lax.all_gather(columns_here, 'gx', axis=0, tiled=True)  256 us
    psum x1, waiting for transfers between devices, local(): square = lax.psum(partial_square, 'gz')  99.3 us
    scatter-add x6, other arithmetic, product_two(): summed = summed.at[:, panel_columns[:, column_slot], :].add(product)  82 us
    all_to_all x1, blocking collectives, sent_and_summed(): lax.all_to_all(tiles, axis, split_axis=0, concat_axis=0, tiled=True)  30.4 us
    dot_general x6, matrix products, product_one(): jnp.einsum('rix,iyx->riy', picked, panel_tiles[:, column_slot], preferred...  28.3 us
    all_gather x2, blocking collectives, picked_2(): lax.all_gather(x, axis)  23.7 us
    dot_general x6, matrix products, product_two(): jnp.einsum('rix,ixy->riy', rounded, panel_tiles[:, column_slot], preferre...  18.8 us
    gather x6, local copies, waits for them, and re-layouts, product_one(): picked = jnp.take(left_panel, panel_columns[:, column_slot], axis=1)  12.9 us
  transfers between devices with their start and end apart: 2, of which 1 were waited for; matrix products, arithmetic and copies ran while one was open for 3% of the time, Pallas kernels for 0%

profile of v1, /device:TPU:32, one launch (start us, length us, event | category | flops | bytes accessed | tf_op | source)
XLA Modules:
  0.0 617.6 jit_solution(18401325591720764018)
XLA Ops:
  6.5 1.2 copy.30
  7.7 7.7 %stack.3 = bf16[16,4,6,128,128]{4,3,1,2,0:T(8,128)(2,1)} broadcast(bf16[4,6,128,128]{3,2,0,1:T(8,128)(2,1)S(1)} %copy.30), dimensions={1,2,3,4} | broadcast | bytes 13369344 | tf_op jit(solution)/shard_map/stack | solution.py:10
  15.4 8.7 %all-to-all-start = ((bf16[16,4,6,128,128]{4,3,1,2,0:T(8,128)(2,1)}), bf16[16,4,6,128,128]{4,3,1,2,0:T(8,128)(2,1)}, u32[]{:S(2)}, u32[]{:S(2)}) async-start(bf16[16,4,6,128,128]{4,3,1,2,0:T(8,128)(2,1)} %stack.3), calls=%async_computation | async-start | bytes 25165824 | tf_op jit(solution)/shard_map/all_to_all | solution.py:11
  24.1 0.0 all-reduce.2.cloned.1.call-start
  24.2 9.7 %all-gather = s32[4,1,1,6]{3,2,1,0:T(1,128)S(1)} all-gather(s32[1,1,1,6]{3,2,1,0:T(1,128)S(1)} %slice-done), channel_id=2, replica_groups=mesh['gx'=16,'gy'=4,'gz'=4] {'gy'}, dimensions={0}, use_global_device_ids=true | all-gather | bytes 120 | tf_op jit(solution)/shard_map/all_gather | solution.py:16
  33.9 0.9 slice.59
  34.8 13.9 %all-gather.1 = bf16[4,1,1,6,128,128]{5,4,3,2,1,0:T(8,128)(2,1)S(1)} all-gather(bf16[1,1,1,6,128,128]{5,4,3,2,1,0:T(8,128)(2,1)S(1)} %slice.59), channel_id=3, replica_groups=mesh['gx'=16,'gy'=4,'gz'=4] {'gy'}, dimensions={0}, use_global_device_ids=true | all-gather | bytes 983040 | tf_op jit(solution)/shard_map/all_gather | solution.py:16
  48.8 0.8 convert_bitcast_fusion
  49.6 1.4 copy.29
  51.0 256.0 %all-gather.2 = s32[1,64,1,6]{3,2,0,1:T(1,128)S(1)} all-gather(s32[1,4,1,6]{3,2,0,1:T(1,128)S(1)} %bitcast.101), channel_id=4, replica_groups=mesh['gx'=16,'gy'=4,'gz'=4] {'gx'}, dimensions={1}, use_global_device_ids=true | all-gather | bytes 1632 | tf_op jit(solution)/shard_map/all_gather | solution.py:78
  307.0 0.4 fusion.41
  307.5 2.2 gather_fusion.4
  309.7 2.1 gather_fusion.3
  311.8 2.2 gather_fusion.2
  314.0 2.1 gather_fusion
  316.1 2.2 gather_fusion.1
  318.3 2.1 gather_fusion.5
  320.5 0.0 all-to-all-done
  320.5 6.6 %copy.31 = bf16[16,4,6,128,128]{4,3,1,0,2:T(8,128)(2,1)S(1)} copy(bf16[16,4,6,128,128]{4,3,1,2,0:T(8,128)(2,1)} %all-to-all-done) | data formatting | bytes 25165824 | tf_op jit(solution)/shard_map/all_to_all | solution.py:11
  327.1 0.0 copy-start
  327.2 3.6 fusion.2
  330.8 3.8 fusion.4
  334.5 3.6 fusion.6
  338.2 3.6 fusion.10
  341.8 3.6 fusion.8
  345.4 10.1 %add_add_fusion = f32[64,128,128]{1,2,0:T(8,128)} fusion(f32[64,128,128]{1,2,0:T(8,128)} %fusion.2, f32[64,128,128]{1,2,0:T(8,128)} %fusion.4, f32[64,128,128]{1,2,0:T(8,128)} %fusion.6, f32[64,128,128]{1,2,0:T(8,128)} %fusion.10, f32[64,128,128]{1,2,0:T(8,128)} %fusion.8, bf16[64,128,128]{2,1,0:T(8,128)(2,1)S(1)} %copy-done.7, ...), kind=kOutput, calls=%fused_computation.15 | convolution fusion | flops 274726912 | bytes 29360640 | tf_op jit(solution)/shard_map/rix,iyx->riy/dot_general | solution.py:48
  355.5 0.0 all-reduce.2.cloned.1.call-update
  355.5 99.3 %all-reduce.2.cloned.1.call-done = f32[128,8192]{0,1:T(8,128)} async-done(((f32[128,8192]{0,1:T(8,128)}), f32[128,8192]{0,1:T(8,128)}) %all-reduce.2.cloned.1.call-update) | async-done | bytes 4194320 | tf_op jit(solution)/shard_map/psum | solution.py:82
  454.8 2.5 convert_element_type.27
  457.4 4.7 fusion.24
  462.1 2.8 fusion.25
  464.9 2.8 fusion.26
  467.7 2.8 fusion.27
  470.6 2.8 fusion.28
  473.4 2.8 fusion.29
  476.2 2.5 broadcast_in_dim.11
  478.6 13.7 %scatter_fusion = f32[128,64,128]{2,0,1:T(8,128)} fusion(f32[128,64,128]{2,0,1:T(8,128)} %broadcast_in_dim.11, s32[64]{0:T(128)S(1)} %get-tuple-element.7, f32[64,128,128]{2,1,0:T(8,128)} %fusion.24), kind=kCustom, calls=%fused_computation.6 | custom fusion | flops 1048576 | bytes 12583168 | tf_op jit(solution)/shard_map/scatter-add | solution.py:60
  492.3 13.7 %scatter_fusion.1 = f32[128,64,128]{2,0,1:T(8,128)} fusion(f32[128,64,128]{2,0,1:T(8,128)} %scatter_fusion, s32[64]{0:T(128)S(1)} %get-tuple-element.8, f32[64,128,128]{2,1,0:T(8,128)} %fusion.25), kind=kCustom, calls=%fused_computation.7 | custom fusion | flops 1048576 | bytes 12583168 | tf_op jit(solution)/shard_map/scatter-add | solution.py:60
  506.1 13.7 %scatter_fusion.2 = f32[128,64,128]{2,0,1:T(8,128)} fusion(f32[128,64,128]{2,0,1:T(8,128)} %scatter_fusion.1, s32[64]{0:T(128)S(1)} %get-tuple-element.9, f32[64,128,128]{2,1,0:T(8,128)} %fusion.26), kind=kCustom, calls=%fused_computation.8 | custom fusion | flops 1048576 | bytes 12583168 | tf_op jit(solution)/shard_map/scatter-add | solution.py:60
  519.8 13.6 %scatter_fusion.3 = f32[128,64,128]{2,0,1:T(8,128)} fusion(f32[128,64,128]{2,0,1:T(8,128)} %scatter_fusion.2, s32[64]{0:T(128)S(1)} %get-tuple-element.10, f32[64,128,128]{2,1,0:T(8,128)} %fusion.27), kind=kCustom, calls=%fused_computation.9 | custom fusion | flops 1048576 | bytes 12583168 | tf_op jit(solution)/shard_map/scatter-add | solution.py:60
  533.3 13.7 %scatter_fusion.4 = f32[128,64,128]{2,0,1:T(8,128)} fusion(f32[128,64,128]{2,0,1:T(8,128)} %scatter_fusion.3, s32[64]{0:T(128)S(1)} %get-tuple-element.11, f32[64,128,128]{2,1,0:T(8,128)} %fusion.28), kind=kCustom, calls=%fused_computation.10 | custom fusion | flops 1048576 | bytes 12583168 | tf_op jit(solution)/shard_map/scatter-add | solution.py:60
  547.0 13.6 %scatter_fusion.5 = f32[128,64,128]{2,0,1:T(8,128)} fusion(f32[128,64,128]{2,0,1:T(8,128)} %scatter_fusion.4, s32[64]{0:T(128)S(1)} %get-tuple-element.6, f32[64,128,128]{2,1,0:T(8,128)} %fusion.29), kind=kCustom, calls=%fused_computation.11 | custom fusion | flops 1048576 | bytes 12583168 | tf_op jit(solution)/shard_map/scatter-add | solution.py:60
  560.6 4.7 broadcast_multiply_fusion
  565.4 5.6 copy.43
  571.0 5.2 fusion
  576.2 2.9 copy.44
  579.1 30.4 %all_to_all.10 = bf16[4,32,8192]{2,1,0:T(8,128)(2,1)S(1)} all-to-all(bf16[4,32,8192]{2,1,0:T(8,128)(2,1)S(1)} %bitcast.98), channel_id=1, replica_groups=mesh['gx'=16,'gy'=4,'gz'=4] {'gy'}, dimensions={0} | all-to-all | bytes 4194304 | tf_op jit(solution)/shard_map/all_to_all | solution.py:27
  609.5 1.3 convert_reduce_fusion
  (33 shorter events, 0.1 us)
Async XLA Ops:
  15.4 8.8 %slice-start = ((s32[1,4,1,6]{3,2,1,0:T(1,128)}), s32[1,1,1,6]{3,2,1,0:T(1,128)S(1)}, s32[]{:S(2)}) async-start(s32[1,4,1,6]{3,2,1,0:T(1,128)} %param.5), calls=%async_computation.3 | async-start | bytes 1024 | tf_op jit(solution)/shard_map/slice | solution.py:71
  15.4 305.1 %all-to-all-start = ((bf16[16,4,6,128,128]{4,3,1,2,0:T(8,128)(2,1)}), bf16[16,4,6,128,128]{4,3,1,2,0:T(8,128)(2,1)}, u32[]{:S(2)}, u32[]{:S(2)}) async-start(bf16[16,4,6,128,128]{4,3,1,2,0:T(8,128)(2,1)} %stack.3), calls=%async_computation | async-start | bytes 25165824 | tf_op jit(solution)/shard_map/all_to_all | solution.py:11
  24.1 26.9 %copy-start.8 = (s32[1,4,1,6]{3,2,1,0:T(1,128)S(1)}, s32[1,4,1,6]{3,2,1,0:T(1,128)}, u32[]{:S(2)}) copy-start(s32[1,4,1,6]{3,2,1,0:T(1,128)} %param.5) | copy-start | bytes 292
  24.1 430.7 %all-reduce.2.cloned.1.call-start = ((), (), s32[]{:S(2)}) async-start(), calls=%async_computation.2 | async-start | bytes 8388608 | tf_op jit(solution)/shard_map/psum | solution.py:82
  320.5 6.7 %copy-start.2 = (bf16[64,128,128]{2,1,0:T(8,128)(2,1)S(1)}, bf16[64,128,128]{2,1,0:T(8,128)(2,1)}, u32[]{:S(2)}) copy-start(bf16[64,128,128]{2,1,0:T(8,128)(2,1)} %gather_fusion.4) | copy-start | bytes 6291460
  327.1 18.2 %copy-start = (bf16[16,4,6,128,128]{4,3,1,0,2:T(8,128)(2,1)}, bf16[16,4,6,128,128]{4,3,1,0,2:T(8,128)(2,1)S(1)}, u32[]{:S(2)}) copy-start(bf16[16,4,6,128,128]{4,3,1,0,2:T(8,128)(2,1)S(1)} %copy.31) | copy-start | bytes 37748740
  327.2 3.6 copy-start.3
  330.8 3.8 copy-start.4
  334.5 3.6 copy-start.5
  338.2 3.6 copy-start.6
  341.8 3.6 copy-start.7
  454.8 7.3 %copy-start.1 = (bf16[16,4,6,128,128]{4,3,1,0,2:T(8,128)(2,1)S(1)}, bf16[16,4,6,128,128]{4,3,1,0,2:T(8,128)(2,1)}, u32[]{:S(2)}) copy-start(bf16[16,4,6,128,128]{4,3,1,0,2:T(8,128)(2,1)} %copy-done) | copy-start | bytes 37748740
Sparse Core Ops, SparseCore 0:
  355.7 99.1 all-reduce.1
